TPU v7x, 32 devices: a whole 2x2x4 slice. The times are simulated.
32 devices in a mesh: col: 4 (over z), row: 8 (over y, x, core).
Axes of the slice: x: 2, y: 2, z: 4, core: 2. Of those that a mesh axis runs over, the one named last changes fastest.
Arguments:
- queries: bfloat16 [32768, 256], P(('col', 'row')), may hold values from -6 to 6
- keys: bfloat16 [32768, 256], P(('col', 'row')), may hold values from -6 to 6
- values: bfloat16 [32768, 256], P(('col', 'row')), may hold values from -6 to 6
- out_grad: bfloat16 [32768, 256], P(('col', 'row')), may hold values from -6 to 6
- weight_table: float32 [64, 2, 21], replicated, may hold values from 0.25 to 2
- profile: int32 [32768], P(('col', 'row')), may hold values from 0 to 63
Outputs:
- output: float32 [32768, 256], P(('col', 'row'))
- query_grad: float32 [32768, 256], P(('col', 'row'))
- key_grad: float32 [32768, 256], P(('col', 'row'))
- value_grad: float32 [32768, 256], P(('col', 'row'))
All inputs are finite; a program needn't handle non-finite values.
Results may differ from a plain program's by a relative error of at most 0.0034.
Values sent between devices are 32-bit elements; how exact they have to be, the bound alone decides.
A program may use at most 128 MiB of HBM per device.

v0:
```python
import math

import jax
import jax.numpy as jnp
from jax import lax
from jax.sharding import PartitionSpec as P

HIGHEST_PRECISION = lax.Precision.HIGHEST


def from_partner(x, axis, distance):
    return lax.ppermute(x, axis, [(i, i ^ 1 << distance) for i in range(lax.axis_size(axis))])


def digit_count(numbers, count):
    total = jnp.zeros_like(numbers)
    for digit_place in range(count):
        total = total + (numbers >= 1 << digit_place).astype(jnp.int32)
    return total


def level_weights(weight_table, profile, head_width):
    table_rows = weight_table.shape[0]
    onehot = (profile[:, None] == jnp.arange(table_rows, dtype=jnp.int32)[None, :]).astype(
        jnp.float32
    )
    flat_table = weight_table.reshape(table_rows, -1)
    picked = jnp.dot(
        onehot, flat_table, precision=HIGHEST_PRECISION, preferred_element_type=jnp.float32
    )
    picked = picked.reshape(profile.shape[0], weight_table.shape[1], weight_table.shape[2])
    depth = jnp.arange(weight_table.shape[2], dtype=jnp.float32)
    scaling = jnp.exp2(-0.5 * depth) / math.sqrt(head_width)
    return picked * scaling


def upper_half(own_index, bit_place):
    return (own_index >> bit_place & 1).astype(jnp.float32)


def sibling_from(gathered, own_index, bit_place):
    member = jnp.arange(gathered.shape[0], dtype=jnp.int32)
    same_group = member >> bit_place + 1 == own_index >> bit_place + 1
    other_half = member >> bit_place & 1 != own_index >> bit_place & 1
    chosen = (same_group & other_half).reshape((gathered.shape[0],) + (1,) * (gathered.ndim - 1))
    return jnp.sum(jnp.where(chosen, gathered, 0.0), axis=0)


def fenwick_states(tile_state, grad_state, row_bits, col_bits):
    row_index = lax.axis_index("row")
    col_index = lax.axis_index("col")
    buckets = []
    pulled = jnp.zeros_like(tile_state)
    carried = tile_state
    stacked = grad_state
    for bit_place in range(row_bits):
        other_carried, other_stack = from_partner((carried, stacked), "row", bit_place)
        upper = upper_half(row_index, bit_place)
        buckets.append(upper * other_carried)
        pulled = pulled + (1.0 - upper) * other_stack[0]
        carried = carried + other_carried
        stacked = stacked[1:] + other_stack[1:]
    group_state, group_grad = (
        lax.all_gather(carried[None], "col", axis=0, tiled=True),
        lax.all_gather(stacked[None], "col", axis=0, tiled=True),
    )
    for bit_place in range(col_bits):
        upper = upper_half(col_index, bit_place)
        buckets.append(upper * sibling_from(group_state, col_index, bit_place))
        pulled = pulled + (1.0 - upper) * sibling_from(
            group_grad[:, bit_place], col_index, bit_place
        )
    return (jnp.stack(buckets, axis=0), pulled)


def local_attention(query_heads, key_heads, value_heads, grad_heads, weights, tile_bits):
    token_count = query_heads.shape[0]
    head_count = query_heads.shape[1]
    span = min(token_count, 512)
    out_parts = []
    query_parts = []
    key_total = jnp.zeros(key_heads.shape, jnp.float32)
    value_total = jnp.zeros(value_heads.shape, jnp.float32)
    for block_start in range(0, token_count, span):
        block_end = block_start + span
        row_places = jnp.arange(block_start, block_end, dtype=jnp.int32)
        col_places = jnp.arange(block_end, dtype=jnp.int32)
        levels = digit_count(jnp.bitwise_xor(row_places[:, None], col_places[None, :]), tile_bits)
        causal = col_places[None, :] <= row_places[:, None]
        block_weights = weights[block_start:block_end]
        level_mask = jnp.zeros((head_count, span, block_end), jnp.float32)
        for level in range(tile_bits + 1):
            level_mask = level_mask + jnp.where(
                levels[None] == level, jnp.transpose(block_weights[:, :, level])[:, :, None], 0.0
            )
        level_mask = jnp.where(causal[None], level_mask, 0.0)
        query_block = query_heads[block_start:block_end]
        grad_block = grad_heads[block_start:block_end]
        key_front = key_heads[:block_end]
        value_front = value_heads[:block_end]
        scores = jnp.einsum(
            "thd,shd->hts", query_block, key_front, preferred_element_type=jnp.float32
        )
        local_probs = (scores * level_mask).astype(jnp.bfloat16)
        out_parts.append(
            jnp.einsum("hts,she->the", local_probs, value_front, preferred_element_type=jnp.float32)
        )
        grad_scores = jnp.einsum(
            "the,she->hts", grad_block, value_front, preferred_element_type=jnp.float32
        )
        local_grad = (grad_scores * level_mask).astype(jnp.bfloat16)
        query_parts.append(
            jnp.einsum("hts,shd->thd", local_grad, key_front, preferred_element_type=jnp.float32)
        )
        key_total = key_total.at[:block_end].add(
            jnp.einsum("hts,thd->shd", local_grad, query_block, preferred_element_type=jnp.float32)
        )
        value_total = value_total.at[:block_end].add(
            jnp.einsum("hts,the->she", local_probs, grad_block, preferred_element_type=jnp.float32)
        )
    return (
        jnp.concatenate(out_parts, axis=0),
        jnp.concatenate(query_parts, axis=0),
        key_total,
        value_total,
    )


def shards(queries, keys, values, out_grad, weight_table, profile):
    token_count = queries.shape[0]
    head_count = weight_table.shape[1]
    head_width = queries.shape[1] // head_count
    tile_bits = token_count.bit_length() - 1
    row_bits = lax.axis_size("row").bit_length() - 1
    col_bits = lax.axis_size("col").bit_length() - 1
    far_levels = row_bits + col_bits
    weights = level_weights(weight_table, profile, head_width)
    far_weights = weights[:, :, tile_bits + 1 : tile_bits + 1 + far_levels]
    head_shape = (token_count, head_count, head_width)
    query_heads = queries.reshape(head_shape)
    key_heads = keys.reshape(head_shape)
    value_heads = values.reshape(head_shape)
    grad_heads = out_grad.reshape(head_shape)
    tile_state = jnp.einsum(
        "thd,the->hde", key_heads, value_heads, preferred_element_type=jnp.float32
    )
    weighted = (query_heads.astype(jnp.float32)[:, :, None, :] * far_weights[..., None]).astype(
        jnp.bfloat16
    )
    grad_state = jnp.einsum(
        "thld,the->lhde", weighted, grad_heads, preferred_element_type=jnp.float32
    )
    local_out, local_dq, local_dk, local_dv = local_attention(
        query_heads, key_heads, value_heads, grad_heads, weights, tile_bits
    )
    bucket, pulled = fenwick_states(tile_state, grad_state, row_bits, col_bits)
    bucket_half = bucket.astype(jnp.bfloat16)
    pulled_half = pulled.astype(jnp.bfloat16)
    reach = jnp.einsum(
        "thd,lhde->thle", query_heads, bucket_half, preferred_element_type=jnp.float32
    )
    far_out = jnp.sum(reach * far_weights[..., None], axis=2)
    back = jnp.einsum("the,lhde->thld", grad_heads, bucket_half, preferred_element_type=jnp.float32)
    far_dq = jnp.sum(back * far_weights[..., None], axis=2)
    far_dk = jnp.einsum(
        "the,hde->thd", value_heads, pulled_half, preferred_element_type=jnp.float32
    )
    far_dv = jnp.einsum("thd,hde->the", key_heads, pulled_half, preferred_element_type=jnp.float32)
    flat_shape = (token_count, head_count * head_width)
    output = (local_out + far_out).reshape(flat_shape)
    query_grad = (local_dq + far_dq).reshape(flat_shape)
    key_grad = (local_dk + far_dk).reshape(flat_shape)
    value_grad = (local_dv + far_dv).reshape(flat_shape)
    return (output, query_grad, key_grad, value_grad)


def solution(mesh):
    in_specs = (
        P(("col", "row"), None),
        P(("col", "row"), None),
        P(("col", "row"), None),
        P(("col", "row"), None),
        P(),
        P(("col", "row")),
    )
    out_specs = (
        P(("col", "row"), None),
        P(("col", "row"), None),
        P(("col", "row"), None),
        P(("col", "row"), None),
    )
    return jax.shard_map(shards, mesh=mesh, in_specs=in_specs, out_specs=out_specs, check_vma=False)
```

profile of v0, /device:TPU:0, one launch (start us, length us, event | category | flops | bytes accessed | tf_op | source)
XLA Modules:
  0.0 149.0 jit_solution(16656411847094975966)
XLA Ops:
  8.6 2.2 %fusion.34 = f32[2,128,128]{2,1,0:T(8,128)} fusion(bf16[1024,2,128]{0,2,1:T(8,128)(2,1)S(1)} %bitcast.271, bf16[1024,256]{1,0:T(8,128)(2,1)} %param.20), kind=kOutput, calls=%fused_computation.69 | convolution fusion | flops 67108864 | bytes 1179648 | tf_op jit(solution)/shard_map/thd,the->hde/dot_general | solution.py:144
  12.4 1.7 %fusion.19 = f32[5,2,128,128]{3,2,0,1:T(8,128)} fusion(f32[1024,2,128]{0,2,1:T(8,128)S(1)} %convert_element_type.1211, f32[1024,2,5]{0,2,1:T(8,128)S(1)} %slice.310, bf16[1024,2,128,1]{2,1,0,3:T(2,128)(2,1)S(1)} %bitcast.278), kind=kOutput, calls=%fused_computation.35 | convolution fusion | flops 338165760 | bytes 2269184 | tf_op jit(solution)/shard_map/thld,the->lhde/dot_general | solution.py:150
  23.9 6.2 %iota_compare_fusion = (pred[512,1024]{1,0:T(8,128)(4,1)S(1)}, pred[512,1024]{1,0:T(8,128)(4,1)S(1)}, pred[512,1024]{1,0:T(8,128)(4,1)S(1)}, pred[512,1024]{1,0:...) fusion(s32[512]{0:T(512)S(1)} %iota_add_fusion), kind=kLoop, calls=%fused_computation.24 | loop fusion | flops 22020096 | bytes 6293504 | tf_op jit(solution)/shard_map/le | solution.py:89
  30.2 7.2 %add_select_fusion = f32[2,512,1024]{2,1,0:T(8,128)S(1)} fusion(f32[2,512]{1,0:T(2,128)S(1)} %get-tuple-element.126, f32[2,512]{1,0:T(2,128)S(1)} %get-tuple-element.127, f32[2,512]{1,0:T(2,128)S(1)} %get-tuple-element.128, f32[2,512]{1,0:T(2,128)S(1)} %get-tuple-element.129, f32[2,512]{1,0:T(2,128)S(1)} %get-tuple-element.130, ...), kind=kLoop, calls=%fused_computation.7 | loop fusion | flops 23068672 | bytes 10530816 | tf_op jit(solution)/shard_map/jit(_where)/select_n | solution.py:96
  40.7 3.4 %add_select_fusion.1 = f32[2,512,512]{2,1,0:T(8,128)S(1)} fusion(f32[2,512]{1,0:T(2,128)S(1)} %get-tuple-element.137, f32[2,512]{1,0:T(2,128)S(1)} %get-tuple-element.138, f32[2,512]{1,0:T(2,128)S(1)} %get-tuple-element.139, f32[2,512]{1,0:T(2,128)S(1)} %get-tuple-element.140, f32[2,512]{1,0:T(2,128)S(1)} %get-tuple-element.141, ...), kind=kLoop, calls=%fused_computation.26 | loop fusion | flops 11534336 | bytes 5287936 | tf_op jit(solution)/shard_map/jit(_where)/select_n | solution.py:96
  47.2 1.8 %copy.157 = bf16[512,256]{0,1:T(8,128)(2,1)} copy(bf16[512,256]{1,0:T(8,128)(2,1)} %get-tuple-element.89) | data formatting | bytes 524288
  49.0 2.7 %fusion.17 = f32[1024,2,128]{0,2,1:T(8,128)} fusion(bf16[512,2,128]{0,2,1:T(8,128)(2,1)} %bitcast.265, bf16[2,512,1024]{2,1,0:T(8,128)(2,1)S(1)} %multiply_convert_fusion.1, f32[512,2,128]{0,2,1:T(8,128)} %convolution_bitcast_fusion.5), kind=kOutput, calls=%fused_computation.33 | convolution fusion | flops 268697600 | bytes 3932160 | tf_op jit(solution)/shard_map/hts,thd->shd/dot_general | solution.py:116
  52.3 1.7 %slice_add_fusion = f32[4,2,128,128]{3,2,0,1:T(8,128)S(1)} fusion(f32[5,2,128,128]{3,2,0,1:T(8,128)} %collective-permute-done.3, f32[5,2,128,128]{3,2,0,1:T(8,128)} %fusion.19), kind=kLoop, calls=%fused_computation.79 | loop fusion | flops 131072 | bytes 1572864 | tf_op jit(solution)/shard_map/add | solution.py:62
  53.9 3.0 %collective-permute-start.4 = (f32[4,2,128,128]{3,2,0,1:T(8,128)S(1)}, f32[4,2,128,128]{3,2,0,1:T(8,128)S(1)}, u32[]{:S(2)}, u32[]{:S(2)}) collective-permute-start(f32[4,2,128,128]{3,2,0,1:T(8,128)S(1)} %slice_add_fusion), channel_id=1, source_target_pairs={{0,2},{1,3},{2,0},{3,1},{4,6},{5,7},{6,4},{7,5},{8,10},{9,11},{10,... | collective-permute-start | bytes 1572872 | tf_op jit(solution)/shard_map/ppermute | solution.py:12
  57.0 1.7 %fusion.78 = f32[2,512,128]{1,2,0:T(8,128)} fusion(bf16[2,512,1024]{2,1,0:T(8,128)(2,1)S(1)} %multiply_convert_fusion.1, bf16[1024,2,128]{0,2,1:T(8,128)(2,1)S(1)} %bitcast.272), kind=kOutput, calls=%fused_computation.166 | convolution fusion | flops 268435456 | bytes 3145728 | tf_op jit(solution)/shard_map/hts,shd->thd/dot_general | solution.py:113
  59.4 9.6 %collective-permute-done.4 = f32[4,2,128,128]{3,2,0,1:T(8,128)S(1)} collective-permute-done((f32[4,2,128,128]{3,2,0,1:T(8,128)S(1)}, f32[4,2,128,128]{3,2,0,1:T(8,128)S(1)}, u32[]{:S(2)}, u32[]{:S(2)}) %collective-permute-start.4) | collective-permute-done | bytes 524320 | tf_op jit(solution)/shard_map/ppermute | solution.py:12
  69.1 1.8 %collective-permute-start.5 = (f32[3,2,128,128]{3,2,0,1:T(8,128)S(1)}, f32[3,2,128,128]{3,2,0,1:T(8,128)S(1)}, u32[]{:S(2)}, u32[]{:S(2)}) collective-permute-start(f32[3,2,128,128]{3,2,0,1:T(8,128)S(1)} %slice_add_fusion.1), channel_id=1, source_target_pairs={{0,4},{1,5},{2,6},{3,7},{4,0},{5,1},{6,2},{7,3},{8,12},{9,13},{10,... | collective-permute-start | bytes 1179656 | tf_op jit(solution)/shard_map/ppermute | solution.py:12
  72.7 6.9 %collective-permute-done.5 = f32[3,2,128,128]{3,2,0,1:T(8,128)S(1)} collective-permute-done((f32[3,2,128,128]{3,2,0,1:T(8,128)S(1)}, f32[3,2,128,128]{3,2,0,1:T(8,128)S(1)}, u32[]{:S(2)}, u32[]{:S(2)}) %collective-permute-start.5) | collective-permute-done | bytes 393248 | tf_op jit(solution)/shard_map/ppermute | solution.py:12
  90.3 3.5 %collective-permute-done.1 = f32[2,128,128]{2,1,0:T(8,128)S(1)} collective-permute-done((f32[2,128,128]{2,1,0:T(8,128)S(1)}, f32[2,128,128]{2,1,0:T(8,128)S(1)}, u32[]{:S(2)}, u32[]{:S(2)}) %collective-permute-start.1) | collective-permute-done | bytes 131104 | tf_op jit(solution)/shard_map/ppermute | solution.py:12
  93.8 1.6 %collective-permute-start.2 = (f32[2,128,128]{2,1,0:T(8,128)S(1)}, f32[2,128,128]{2,1,0:T(8,128)S(1)}, u32[]{:S(2)}, u32[]{:S(2)}) collective-permute-start(f32[2,128,128]{2,1,0:T(8,128)S(1)} %add.1243), channel_id=1, source_target_pairs={{0,4},{1,5},{2,6},{3,7},{4,0},{5,1},{6,2},{7,3},{8,12},{9,13},{10,... | collective-permute-start | bytes 393224 | tf_op jit(solution)/shard_map/ppermute | solution.py:12
  95.4 3.4 %collective-permute-done.2 = f32[2,128,128]{2,1,0:T(8,128)S(1)} collective-permute-done((f32[2,128,128]{2,1,0:T(8,128)S(1)}, f32[2,128,128]{2,1,0:T(8,128)S(1)}, u32[]{:S(2)}, u32[]{:S(2)}) %collective-permute-start.2) | collective-permute-done | bytes 131104 | tf_op jit(solution)/shard_map/ppermute | solution.py:12
  98.9 21.5 %all-gather = f32[8,128,128]{2,1,0:T(8,128)S(1)} all-gather(f32[2,128,128]{2,1,0:T(8,128)S(1)} %add.1244), channel_id=2, replica_groups=mesh['col'=4,'row'=8] {'col'}, dimensions={0}, use_global_device_ids=true | all-gather | bytes 655360 | tf_op jit(solution)/shard_map/all_gather | solution.py:64
  124.0 1.9 %fusion.1 = f32[1024,2,128]{0,2,1:T(8,128)} fusion(f32[1024,2,5]{0,2,1:T(8,128)S(1)} %copy-done.48, bf16[1024,2,128,1]{2,1,0,3:T(2,128)(2,1)S(1)} %bitcast.269, bf16[5,2,128,128]{3,2,1,0:T(8,128)(2,1)S(1)} %copy-done.51), kind=kOutput, calls=%fused_computation.3 | convolution fusion | flops 337903616 | bytes 1941504 | tf_op jit(solution)/shard_map/thd,lhde->thle/dot_general | solution.py:159
  125.8 1.6 %copy.94 = f32[1024,256]{1,0:T(8,128)S(1)} copy(f32[1024,256]{0,1:T(8,128)} %bitcast.275) | data formatting | bytes 2097152 | tf_op jit(solution)/shard_map/reduce_sum | solution.py:162
  128.6 2.6 %fusion.15 = f32[1024,2,128]{0,2,1:T(8,128)} fusion(f32[1024,2,128]{0,2,1:T(8,128)} %fusion.17, bf16[2,128,128]{2,1,0:T(8,128)(2,1)S(1)} %fusion.59, bf16[1024,256]{1,0:T(8,128)(2,1)S(1)} %copy-done.8), kind=kOutput, calls=%fused_computation.31 | convolution fusion | flops 67371008 | bytes 2686976 | tf_op jit(solution)/shard_map/the,hde->thd/dot_general | solution.py:165
  131.1 2.5 %copy.113 = f32[1024,256]{1,0:T(8,128)} copy(f32[1024,256]{0,1:T(8,128)} %bitcast.254) | data formatting | bytes 2097152
  133.7 2.6 %fusion.16 = f32[1024,2,128]{0,2,1:T(8,128)} fusion(f32[1024,2,128]{0,2,1:T(8,128)} %fusion.18, bf16[2,128,128]{2,1,0:T(8,128)(2,1)S(1)} %fusion.59, bf16[1024,256]{1,0:T(8,128)(2,1)S(1)} %copy-done.10), kind=kOutput, calls=%fused_computation.32 | convolution fusion | flops 67371008 | bytes 2686976 | tf_op jit(solution)/shard_map/thd,hde->the/dot_general | solution.py:168
  136.3 2.5 %copy.114 = f32[1024,256]{1,0:T(8,128)} copy(f32[1024,256]{0,1:T(8,128)} %bitcast.253) | data formatting | bytes 2097152
  138.8 2.2 %maximum_add_fusion.1 = f32[1024,256]{1,0:T(8,128)} fusion(f32[1024,256]{1,0:T(8,128)S(1)} %copy.106, f32[512,256]{1,0:T(8,128)} %copy.103, f32[512,256]{1,0:T(8,128)S(1)} %copy-done.29), kind=kLoop, calls=%fused_computation.40 | loop fusion | flops 524288 | bytes 3145728 | tf_op jit(solution)/shard_map/add | solution.py:171
  (186 shorter events, 38.3 us)
Async XLA Ops:
  7.2 4.1 %copy-start.52 = (s32[1024]{0:T(1024)S(1)}, s32[1024]{0:T(1024)}, u32[]{:S(2)}) copy-start(s32[1024]{0:T(1024)} %param.23) | copy-start | bytes 12292
  7.2 4.4 %copy-start.22 = (bf16[1024,256]{1,0:T(8,128)(2,1)S(1)}, bf16[1024,256]{1,0:T(8,128)(2,1)}, u32[]{:S(2)}) copy-start(bf16[1024,256]{1,0:T(8,128)(2,1)} %param.18) | copy-start | bytes 1572868
  7.2 113.3 %all-gather.4.cloned.1.call-start = ((), (), s32[]{:S(2)}) async-start(), calls=%async_computation | async-start | bytes 1310720 | tf_op jit(solution)/shard_map/all_gather | solution.py:65
  10.7 77.1 %collective-permute-start = (f32[2,128,128]{2,1,0:T(8,128)}, f32[2,128,128]{2,1,0:T(8,128)S(1)}, u32[]{:S(2)}, u32[]{:S(2)}) collective-permute-start(f32[2,128,128]{2,1,0:T(8,128)} %fusion.34), channel_id=1, source_target_pairs={{0,1},{1,0},{2,3},{3,2},{4,5},{5,4},{6,7},{7,6},{8,9},{9,8},{10,11... | collective-permute-start | bytes 393224 | tf_op jit(solution)/shard_map/ppermute | solution.py:12
  14.1 38.1 %collective-permute-start.3 = (f32[5,2,128,128]{3,2,0,1:T(8,128)}, f32[5,2,128,128]{3,2,0,1:T(8,128)}, u32[]{:S(2)}, u32[]{:S(2)}) collective-permute-start(f32[5,2,128,128]{3,2,0,1:T(8,128)} %fusion.19), channel_id=1, source_target_pairs={{0,1},{1,0},{2,3},{3,2},{4,5},{5,4},{6,7},{7,6},{8,9},{9,8},{10,11... | collective-permute-start | bytes 1966088 | tf_op jit(solution)/shard_map/ppermute | solution.py:12
  15.0 6.8 %slice-start = ((bf16[1024,256]{1,0:T(8,128)(2,1)}), bf16[512,256]{1,0:T(8,128)(2,1)S(1)}, s32[]{:S(2)}) async-start(bf16[1024,256]{1,0:T(8,128)(2,1)} %param.20), calls=%async_computation.1 | async-start | bytes 524288 | tf_op jit(solution)/shard_map/slice | solution.py:100
  23.7 20.4 %copy-start.13 = (bf16[512,256]{0,1:T(8,128)(2,1)}, bf16[512,256]{0,1:T(8,128)(2,1)S(1)}, u32[]{:S(2)}) copy-start(bf16[512,256]{0,1:T(8,128)(2,1)S(1)} %copy.158) | copy-start | bytes 786436
  23.8 13.6 %copy-start.18 = (bf16[512,256]{0,1:T(8,128)(2,1)}, bf16[512,256]{0,1:T(8,128)(2,1)S(1)}, u32[]{:S(2)}) copy-start(bf16[512,256]{0,1:T(8,128)(2,1)S(1)} %copy.159) | copy-start | bytes 786436
  30.2 7.3 %copy-start.6 = (bf16[1024,256]{1,0:T(8,128)(2,1)S(1)}, bf16[1024,256]{1,0:T(8,128)(2,1)}, u32[]{:S(2)}) copy-start(bf16[1024,256]{1,0:T(8,128)(2,1)} %param.20) | copy-start | bytes 1572868
  51.7 5.2 %copy-start.27 = (bf16[1024,256]{0,1:T(8,128)(2,1)S(1)}, bf16[1024,256]{0,1:T(8,128)(2,1)}, u32[]{:S(2)}) copy-start(bf16[1024,256]{0,1:T(8,128)(2,1)} %copy-done.26) | copy-start | bytes 1572868
  51.7 6.9 %copy-start.20 = (bf16[512,256]{0,1:T(8,128)(2,1)S(1)}, bf16[512,256]{0,1:T(8,128)(2,1)}, u32[]{:S(2)}) copy-start(bf16[512,256]{0,1:T(8,128)(2,1)} %copy.157) | copy-start | bytes 786436
  52.2 18.7 %copy-start.4 = (bf16[2,512,512]{2,1,0:T(8,128)(2,1)}, bf16[2,512,512]{2,1,0:T(8,128)(2,1)S(1)}, u32[]{:S(2)}) copy-start(bf16[2,512,512]{2,1,0:T(8,128)(2,1)S(1)} %multiply_convert_fusion.5) | copy-start | bytes 3145732
  52.2 6.4 %copy-start.1 = (f32[2,512,1024]{2,1,0:T(8,128)S(1)}, f32[2,512,1024]{2,1,0:T(8,128)}, u32[]{:S(2)}) copy-start(f32[2,512,1024]{2,1,0:T(8,128)} %copy-done) | copy-start | bytes 12582916
  52.2 6.4 %copy-start.9 = (bf16[1024,256]{1,0:T(8,128)(2,1)S(1)}, bf16[1024,256]{1,0:T(8,128)(2,1)}, u32[]{:S(2)}) copy-start(bf16[1024,256]{1,0:T(8,128)(2,1)} %param.19) | copy-start | bytes 1572868
  53.9 15.1 %collective-permute-start.4 = (f32[4,2,128,128]{3,2,0,1:T(8,128)S(1)}, f32[4,2,128,128]{3,2,0,1:T(8,128)S(1)}, u32[]{:S(2)}, u32[]{:S(2)}) collective-permute-start(f32[4,2,128,128]{3,2,0,1:T(8,128)S(1)} %slice_add_fusion), channel_id=1, source_target_pairs={{0,2},{1,3},{2,0},{3,1},{4,6},{5,7},{6,4},{7,5},{8,10},{9,11},{10,... | collective-permute-start | bytes 1572872 | tf_op jit(solution)/shard_map/ppermute | solution.py:12
  58.6 12.3 %copy-start.14 = (bf16[512,256]{0,1:T(8,128)(2,1)S(1)}, bf16[512,256]{0,1:T(8,128)(2,1)}, u32[]{:S(2)}) copy-start(bf16[512,256]{0,1:T(8,128)(2,1)} %copy-done.13) | copy-start | bytes 786436
  59.4 11.8 %copy-start.19 = (bf16[512,256]{0,1:T(8,128)(2,1)S(1)}, bf16[512,256]{0,1:T(8,128)(2,1)}, u32[]{:S(2)}) copy-start(bf16[512,256]{0,1:T(8,128)(2,1)} %copy-done.18) | copy-start | bytes 786436
  69.1 10.5 %collective-permute-start.5 = (f32[3,2,128,128]{3,2,0,1:T(8,128)S(1)}, f32[3,2,128,128]{3,2,0,1:T(8,128)S(1)}, u32[]{:S(2)}, u32[]{:S(2)}) collective-permute-start(f32[3,2,128,128]{3,2,0,1:T(8,128)S(1)} %slice_add_fusion.1), channel_id=1, source_target_pairs={{0,4},{1,5},{2,6},{3,7},{4,0},{5,1},{6,2},{7,3},{8,12},{9,13},{10,... | collective-permute-start | bytes 1179656 | tf_op jit(solution)/shard_map/ppermute | solution.py:12
  88.8 5.0 %collective-permute-start.1 = (f32[2,128,128]{2,1,0:T(8,128)S(1)}, f32[2,128,128]{2,1,0:T(8,128)S(1)}, u32[]{:S(2)}, u32[]{:S(2)}) collective-permute-start(f32[2,128,128]{2,1,0:T(8,128)S(1)} %add.1242), channel_id=1, source_target_pairs={{0,2},{1,3},{2,0},{3,1},{4,6},{5,7},{6,4},{7,5},{8,10},{9,11},{10,... | collective-permute-start | bytes 393224 | tf_op jit(solution)/shard_map/ppermute | solution.py:12
  90.3 31.7 %copy-start.44 = (bf16[1024,2,128]{2,1,0:T(2,128)(2,1)S(1)}, bf16[1024,2,128]{2,1,0:T(2,128)(2,1)}, u32[]{:S(2)}) copy-start(bf16[1024,2,128]{2,1,0:T(2,128)(2,1)} %copy-done.43) | copy-start | bytes 1572868
  90.3 31.7 %copy-start.48 = (f32[1024,2,5]{0,2,1:T(8,128)S(1)}, f32[1024,2,5]{0,2,1:T(8,128)}, u32[]{:S(2)}) copy-start(f32[1024,2,5]{0,2,1:T(8,128)} %copy-done.47) | copy-start | bytes 122884
  93.8 5.0 %collective-permute-start.2 = (f32[2,128,128]{2,1,0:T(8,128)S(1)}, f32[2,128,128]{2,1,0:T(8,128)S(1)}, u32[]{:S(2)}, u32[]{:S(2)}) collective-permute-start(f32[2,128,128]{2,1,0:T(8,128)S(1)} %add.1243), channel_id=1, source_target_pairs={{0,4},{1,5},{2,6},{3,7},{4,0},{5,1},{6,2},{7,3},{8,12},{9,13},{10,... | collective-permute-start | bytes 393224 | tf_op jit(solution)/shard_map/ppermute | solution.py:12
  128.6 5.1 %copy-start.10 = (bf16[1024,256]{1,0:T(8,128)(2,1)S(1)}, bf16[1024,256]{1,0:T(8,128)(2,1)}, u32[]{:S(2)}) copy-start(bf16[1024,256]{1,0:T(8,128)(2,1)} %param.19) | copy-start | bytes 1572868
  133.7 5.1 %copy-start.29 = (f32[512,256]{1,0:T(8,128)S(1)}, f32[512,256]{1,0:T(8,128)}, u32[]{:S(2)}) copy-start(f32[512,256]{1,0:T(8,128)} %copy.102) | copy-start | bytes 1572868
  (38 other events, 84.6 us)
Sparse Core Ops, SparseCore 0:
  81.3 37.0 all-gather.3
where the time goes:
time: 150 us; the launch traced here: 149 us
  other arithmetic  33.1 us (22%)
  matrix products  24.3 us (16%)
  waiting for transfers between devices  23.5 us (16%)
  local copies, waits for them, and re-layouts  23.1 us (15%)
  blocking collectives  21.5 us (14%)
  between operations  14.9 us (10%)
  starting transfers between devices  8.55 us (6%)
    ppermute x6, waiting for transfers between devices, from_partner(): lax.ppermute(x, axis, [(i, i ^ 1 << distance) for i in range(lax.axis_siz...  23.4 us
    all_gather x1, blocking collectives, fenwick_states(): lax.all_gather(carried[None], 'col', axis=0, tiled=True)  21.5 us
    unnamed x114, local copies, waits for them, and re-layouts  13.4 us
    select_n x2, other arithmetic, local_attention(): level_mask = jnp.where(causal[None], level_mask, 0.0)  10.6 us
    ppermute x6, starting transfers between devices, from_partner(): lax.ppermute(x, axis, [(i, i ^ 1 << distance) for i in range(lax.axis_siz...  8.51 us
    le x2, other arithmetic, local_attention(): causal = col_places[None, :] <= row_places[:, None]  7.28 us
    eq x5, other arithmetic, local_attention(): levels[None] == level  5.67 us
    dot_general x2, matrix products, local_attention(): jnp.einsum('hts,thd->shd', local_grad, query_block, preferred_element_typ...  3.79 us
  transfers between devices with their start and end apart: 7, of which 4 were waited for; matrix products, arithmetic and copies ran while one was open for 35% of the time, Pallas kernels for 0%

commit v1 on v0

v1 whole, which is shorter than its diff:
```python
import functools
import math

import jax
import jax.numpy as jnp
from jax import lax
from jax.experimental import pallas as pl
from jax.experimental.pallas import tpu as pltpu
from jax.sharding import PartitionSpec as P

MESH = pl.DeviceIdType.MESH
F32 = jnp.float32
BF16 = jnp.bfloat16
NN = (((1,), (0,)), ((), ()))
NT = (((1,), (1,)), ((), ()))
TN = (((0,), (0,)), ((), ()))
CHUNK = 128


def mm(a, b, dims):
    return lax.dot_general(a, b, dims, preferred_element_type=F32)


def main_kernel(
    dims,
    q_ref, k_ref, v_ref, g_ref, tab_ref, prof_ref,
    lo_ref, lq_ref, lk_ref, lv_ref, wq_ref, wg_ref, bnt_ref, bnn_ref, pul_ref,
    w_scr, lev_scr, m_scr, p_scr, d_scr,
    st, x0, pin, sum1, ain, b1, b2, tot, zout, zin, far,
    pair_send, pair_recv, red_send, red_recv, z_send, z_recv, ga_send, ga_recv, gb_send, gb_recv,
):
    T, H, D, cols, rows, span = dims
    rows_bits = rows.bit_length() - 1
    col_bits = cols.bit_length() - 1
    L = rows_bits + col_bits
    chips = rows // 2
    qb = rows_bits - 1
    R = D // chips
    tile_bits = T.bit_length() - 1
    span_bits = span.bit_length() - 1
    z = lax.axis_index("col")
    row = lax.axis_index("row")
    core = lax.rem(row, 2)
    chip = lax.div(row, 2)
    other = 1 - core

    def chip_at(offset):
        return lax.rem(chip + offset, chips)

    def col_at(offset):
        return lax.rem(z + offset, cols)

    barrier = pltpu.get_barrier_semaphore()
    pl.semaphore_signal(barrier, inc=1, device_id=(z, chip * 2 + other), device_id_type=MESH)
    for offset in range(1, chips):
        pl.semaphore_signal(
            barrier, inc=1, device_id=(z, chip_at(offset) * 2 + core), device_id_type=MESH
        )
    for offset in range(1, cols):
        pl.semaphore_signal(barrier, inc=1, device_id=(col_at(offset), row), device_id_type=MESH)

    def remote(src, dst, send, recv, device):
        return pltpu.make_async_remote_copy(
            src_ref=src, dst_ref=dst, send_sem=send, recv_sem=recv,
            device_id=device, device_id_type=MESH,
        )

    profiles = tab_ref.shape[0]
    levels = tab_ref.shape[2]
    onehot = jnp.where(
        lax.broadcasted_iota(jnp.int32, (profiles, T), 0) == prof_ref[...], 1.0, 0.0
    ).astype(BF16)
    onehot = jnp.concatenate([onehot, onehot, onehot], axis=0)
    place = lax.broadcasted_iota(jnp.int32, (profiles, levels), 1)
    scale = jnp.zeros((profiles, levels), F32)
    for level in range(levels):
        scale = jnp.where(place == level, 2.0 ** (-0.5 * level) / math.sqrt(D), scale)
    for h in range(H):
        table = tab_ref[:, h, :] * scale
        top = table.astype(BF16)
        rest = table - top.astype(F32)
        mid = rest.astype(BF16)
        low = (rest - mid.astype(F32)).astype(BF16)
        w_scr[h] = mm(onehot, jnp.concatenate([top, mid, low], axis=0), TN)

    def weigh(src, dst, h):
        for start in range(0, T, CHUNK):
            rs = slice(start, start + CHUNK)
            x = src[rs, h * D : (h + 1) * D].astype(F32)
            for j in range(L):
                level = tile_bits + 1 + j
                c = (h * L + j) * D
                dst[rs, c : c + D] = (x * w_scr[h, rs, level : level + 1]).astype(BF16)

    for h in range(H):
        hs = slice(h * D, (h + 1) * D)
        weigh(q_ref, wq_ref, h)
        state = mm(v_ref[:, hs], k_ref[:, hs], TN)
        grads = mm(g_ref[:, hs], wq_ref[:, h * L * D : (h + 1) * L * D], TN)
        st[h, 0] = state
        for j in range(1, L):
            st[h, j] = grads[:, j * D : (j + 1) * D]
        x0[h] = jnp.where(core == 0, state, grads[:, :D])

    pl.semaphore_wait(barrier, chips + cols - 1)
    partner = (z, chip * 2 + other)
    pair = remote(st.at[other], pin, pair_send.at[0], pair_recv.at[0], partner)
    pair.start()
    near = remote(x0, far.at[0], pair_send.at[1], pair_recv.at[1], partner)
    near.start()

    r_at = lax.broadcasted_iota(jnp.int32, (span, span), 0)
    c_at = lax.broadcasted_iota(jnp.int32, (span, span), 1)
    apart = jnp.bitwise_xor(r_at, c_at)
    lev = jnp.zeros((span, span), jnp.int32)
    for bit in range(span_bits):
        lev = lev + jnp.where(apart >= 1 << bit, 1, 0)
    lev_scr[...] = jnp.where(c_at <= r_at, lev, -1)

    last = T // span - 1

    def unit(h, i):
        hs = slice(h * D, (h + 1) * D)
        ts = slice(i * span, (i + 1) * span)
        width = (i + 1) * span
        for start in range(0, span, 64):
            rs = slice(start, start + 64)
            wts = slice(i * span + start, i * span + start + 64)
            mask = jnp.zeros((64, span), F32)
            here = lev_scr[rs, :]
            for level in range(span_bits + 1):
                mask = jnp.where(here == level, w_scr[h, wts, level : level + 1], mask)
            m_scr[rs, :] = mask
        q = q_ref[ts, hs]
        g = g_ref[ts, hs]
        for b in range(i + 1):
            bs = slice(b * span, (b + 1) * span)
            if b < i:
                level = span_bits + (b ^ i).bit_length()
                mask = w_scr[h, ts, level : level + 1]
            else:
                mask = m_scr[...]
            p_scr[:, bs] = (mm(q, k_ref[bs, hs], NT) * mask).astype(BF16)
            d_scr[:, bs] = (mm(g, v_ref[bs, hs], NT) * mask).astype(BF16)
        ws = slice(0, width)
        lo_ref[ts, hs] = mm(p_scr[:, ws], v_ref[ws, hs], NN)
        lq_ref[ts, hs] = mm(d_scr[:, ws], k_ref[ws, hs], NN)
        dk = mm(d_scr[:, ws], q, TN)
        dv = mm(p_scr[:, ws], g, TN)
        if i == last:
            lk_ref[ws, hs] = dk
            lv_ref[ws, hs] = dv
        else:
            lk_ref[ws, hs] += dk
            lv_ref[ws, hs] += dv

    work = [(h, i) for i in range(last, -1, -1) for h in range(H)]
    cut1 = 1
    cut2 = max(cut1, len(work) * 4 // 8)
    cut3 = max(cut2, len(work) * 6 // 8)

    for h, i in work[:cut1]:
        unit(h, i)

    pair.wait()
    for p in range(chips):
        rs = slice(p * R, (p + 1) * R)
        sum1[p] = st[core, :, rs, :] + pin[:, rs, :]
    reduces = []
    for offset in range(1, chips):
        to = chip_at(offset)
        copy = remote(
            sum1.at[to], ain.at[chip], red_send.at[offset], red_recv.at[offset],
            (z, to * 2 + core),
        )
        copy.start()
        reduces.append(copy)
    ain[chip] = sum1[chip]

    for h, i in work[cut1:cut2]:
        unit(h, i)

    for copy in reduces:
        copy.wait()
    tot[0] = sum([ain[p, 0] for p in range(1, chips)], ain[0, 0])
    for jj in range(col_bits):
        tot[1 + jj] = sum([ain[p, 1 + qb + jj] for p in range(1, chips)], ain[0, 1 + qb + jj])

    def sibling(mine, theirs, bit):
        same = lax.div(mine, 2 << bit) == theirs >> bit + 1
        differs = lax.rem(lax.div(mine, 1 << bit), 2) != theirs >> bit & 1
        return jnp.logical_and(same, differs)

    for to in range(cols):
        value = jnp.zeros((R, D), F32)
        for jj in range(col_bits):
            piece = tot[0] if to >> jj & 1 else tot[1 + jj]
            value = jnp.where(sibling(z, to, jj), piece, value)
        zout[to] = value
    crosses = []
    for offset in range(1, cols):
        to = col_at(offset)
        copy = remote(
            zout.at[to], zin.at[z], z_send.at[offset], z_recv.at[offset], (to, row)
        )
        copy.start()
        crosses.append(copy)
    zin[z] = jnp.zeros((R, D), F32)

    mine = pl.ds(pl.multiple_of(chip * R, R), R)
    firsts = []
    if qb:
        for to in range(chips):
            for jj in range(qb):
                source = 0 if to >> jj & 1 else 1 + jj
                group = [
                    p for p in range(chips)
                    if p >> jj + 1 == to >> jj + 1 and (p >> jj & 1) != (to >> jj & 1)
                ]
                b1[to, jj] = sum([ain[p, source] for p in group[1:]], ain[group[0], source])
        for offset in range(1, chips):
            to = chip_at(offset)
            copy = remote(
                b1.at[to], far.at[pl.ds(1, qb), core, mine], ga_send.at[offset],
                ga_recv.at[offset], (z, to * 2 + core),
            )
            copy.start()
            firsts.append(copy)
        for jj in range(qb):
            far[1 + jj, core, mine] = b1[chip, jj]

    for h, i in work[cut2:cut3]:
        unit(h, i)

    for copy in crosses:
        copy.wait()
    for jj in range(col_bits):
        value = jnp.zeros((R, D), F32)
        for source in range(cols):
            value = value + jnp.where(sibling(z, source, jj), zin[source], 0.0)
        b2[jj] = value
    seconds = []
    if col_bits:
        for offset in range(1, chips):
            to = chip_at(offset)
            copy = remote(
                b2, far.at[pl.ds(1 + qb, col_bits), core, mine], gb_send.at[offset],
                gb_recv.at[offset], (z, to * 2 + core),
            )
            copy.start()
            seconds.append(copy)
        for jj in range(col_bits):
            far[1 + qb + jj, core, mine] = b2[jj]
    relays = []
    if qb:
        for copy in firsts:
            copy.wait()
        relay = remote(
            far.at[pl.ds(1, qb), core], far.at[pl.ds(1, qb), core],
            pair_send.at[2], pair_recv.at[2], partner,
        )
        relay.start()
        relays.append(relay)

    for h, i in work[cut3:]:
        unit(h, i)
    for h in range(H):
        weigh(g_ref, wg_ref, h)

    if col_bits:
        for copy in seconds:
            copy.wait()
        relay = remote(
            far.at[pl.ds(1 + qb, col_bits), core], far.at[pl.ds(1 + qb, col_bits), core],
            pair_send.at[3], pair_recv.at[3], partner,
        )
        relay.start()
        relays.append(relay)
    near.wait()
    for relay in relays:
        relay.wait()

    digits = [core]
    digits += [lax.rem(lax.div(chip, 1 << jj), 2) for jj in range(qb)]
    digits += [lax.rem(lax.div(z, 1 << jj), 2) for jj in range(col_bits)]
    for h in range(H):
        pulled = jnp.zeros((D, D), F32)
        for j in range(L):
            value = far[j, h]
            up = digits[j] == 1
            pulled = pulled + jnp.where(up, 0.0, value)
            half = jnp.where(up, value, 0.0).astype(BF16)
            bnt_ref[h, :, j * D : (j + 1) * D] = half
            bnn_ref[h, j * D : (j + 1) * D, :] = half
        pul_ref[h] = pulled.astype(BF16)


def finish_kernel(
    dims, lo, lq, lk, lv, wq, wg, k, v, bnt, bnn, pul, out, dq, dk, dv
):
    H, D, L = dims
    for h in range(H):
        hs = slice(h * D, (h + 1) * D)
        ls = slice(h * L * D, (h + 1) * L * D)
        out[:, hs] = lo[:, hs] + mm(wq[:, ls], bnt[h], NT)
        dq[:, hs] = lq[:, hs] + mm(wg[:, ls], bnn[h], NN)
        dk[:, hs] = lk[:, hs] + mm(v[:, hs], pul[h], NN)
        dv[:, hs] = lv[:, hs] + mm(k[:, hs], pul[h], NT)


def shards(cols, rows, queries, keys, values, out_grad, weight_table, profile):
    T = queries.shape[0]
    H = weight_table.shape[1]
    D = queries.shape[1] // H
    levels = weight_table.shape[2]
    L = rows.bit_length() + cols.bit_length() - 2
    chips = rows // 2
    qb = rows.bit_length() - 2
    col_bits = cols.bit_length() - 1
    R = D // chips
    span = min(T, 256)
    assert H == 2 and R % 8 == 0
    vm = pl.BlockSpec(memory_space=pltpu.VMEM)
    sds = jax.ShapeDtypeStruct
    dma = pltpu.SemaphoreType.DMA
    local = sds((T, H * D), F32)
    weighted = sds((T, H * L * D), BF16)
    parts = pl.pallas_call(
        functools.partial(main_kernel, (T, H, D, cols, rows, span)),
        out_shape=[
            local, local, local, local, weighted, weighted,
            sds((H, D, L * D), BF16), sds((H, L * D, D), BF16), sds((H, D, D), BF16),
        ],
        in_specs=[vm] * 6,
        out_specs=[vm] * 9,
        scratch_shapes=[
            pltpu.VMEM((H, T, levels), F32),
            pltpu.VMEM((span, span), jnp.int32),
            pltpu.VMEM((span, span), F32),
            pltpu.VMEM((span, T), BF16),
            pltpu.VMEM((span, T), BF16),
            pltpu.VMEM((H, L, D, D), F32),
            pltpu.VMEM((H, D, D), F32),
            pltpu.VMEM((L, D, D), F32),
            pltpu.VMEM((chips, L, R, D), F32),
            pltpu.VMEM((chips, L, R, D), F32),
            pltpu.VMEM((chips, max(qb, 1), R, D), F32),
            pltpu.VMEM((max(col_bits, 1), R, D), F32),
            pltpu.VMEM((1 + col_bits, R, D), F32),
            pltpu.VMEM((cols, R, D), F32),
            pltpu.VMEM((cols, R, D), F32),
            pltpu.VMEM((L, H, D, D), F32),
            dma((4,)), dma((4,)),
            dma((chips,)), dma((chips,)),
            dma((cols,)), dma((cols,)),
            dma((chips,)), dma((chips,)),
            dma((chips,)), dma((chips,)),
        ],
        compiler_params=pltpu.CompilerParams(
            collective_id=0, has_side_effects=True, vmem_limit_bytes=40 * 1024 * 1024
        ),
        name="main",
    )(queries, keys, values, out_grad, weight_table, profile.reshape(1, T))
    lo, lq, lk, lv, wq, wg, bnt, bnn, pul = parts
    block = min(T, 256)
    tile = pl.BlockSpec((block, H * D), lambda i: (i, 0))
    wide = pl.BlockSpec((block, H * L * D), lambda i: (i, 0))
    whole = lambda s: pl.BlockSpec(s, lambda i: (0, 0, 0))
    return pl.pallas_call(
        functools.partial(finish_kernel, (H, D, L)),
        grid=(T // block,),
        out_shape=[local] * 4,
        in_specs=[tile] * 4 + [wide] * 2 + [tile] * 2
        + [whole((H, D, L * D)), whole((H, L * D, D)), whole((H, D, D))],
        out_specs=[tile] * 4,
        compiler_params=pltpu.CompilerParams(vmem_limit_bytes=24 * 1024 * 1024),
        name="finish",
    )(lo, lq, lk, lv, wq, wg, keys, values, bnt, bnn, pul)


def solution(mesh):
    tokens = P(("col", "row"), None)
    return jax.shard_map(
        functools.partial(shards, mesh.shape["col"], mesh.shape["row"]),
        mesh=mesh,
        in_specs=(tokens,) * 4 + (P(), P(("col", "row"))),
        out_specs=(tokens,) * 4,
        check_vma=False,
    )
```

time: 150 us -> 32.3 us (0.22)
  other arithmetic: 33.1 us -> 0 us
  Pallas kernels: 0 us -> 25.5 us
  matrix products: 24.3 us -> 0 us
  waiting for transfers between devices: 23.5 us -> 0 us
  blocking collectives: 21.5 us -> 0 us
  local copies, waits for them, and re-layouts: 23.1 us -> 5.68 us
  between operations: 14.9 us -> 0.65 us
  starting transfers between devices: 8.55 us -> 0 us
    pallas_call x0 -> x2, Pallas kernels: none -> 25.5 us  [the longest x1 22 us: shards(): pl.pallas_call(functools.partial(main_kernel, (T, H, D, cols, rows, span)...]
    dot_general x19 -> x0, matrix products: 24.3 us -> none  [the longest x2 3.79 us: local_attention(): jnp.einsum('hts,thd->shd', local_grad, query_block, preferred_element_typ...]
    ppermute x6 -> x0, waiting for transfers between devices: 23.4 us -> none  [from_partner(): lax.ppermute(x, axis, [(i, i ^ 1 << distance) for i in range(lax.axis_siz...]
    all_gather x1 -> x0, blocking collectives: 21.5 us -> none  [fenwick_states(): lax.all_gather(carried[None], 'col', axis=0, tiled=True)]
    select_n x2 -> x0, other arithmetic: 10.6 us -> none  [local_attention(): level_mask = jnp.where(causal[None], level_mask, 0.0)]
    ppermute x6 -> x0, starting transfers between devices: 8.51 us -> none  [from_partner(): lax.ppermute(x, axis, [(i, i ^ 1 << distance) for i in range(lax.axis_siz...]
    unnamed x114 -> x11, local copies, waits for them, and re-layouts: 13.4 us -> 5.68 us
    le x2 -> x0, other arithmetic: 7.28 us -> none  [local_attention(): causal = col_places[None, :] <= row_places[:, None]]
  transfers between devices with their start and end apart: 7 -> 0, of which waited for: 4 -> 0; matrix products, arithmetic and copies ran while one was open for 35% -> 0% of each run, Pallas kernels for 0% -> 0%
where the time goes in v1:
time: 32.3 us; the launch traced here: 31.9 us
  Pallas kernels  25.5 us (79%)
  local copies, waits for them, and re-layouts  5.68 us (18%)
  between operations  0.65 us (2%)
    pallas_call x1, Pallas kernels, shards(): pl.pallas_call(functools.partial(main_kernel, (T, H, D, cols, rows, span)...  22 us
    unnamed x11, local copies, waits for them, and re-layouts  5.68 us
    pallas_call x1, Pallas kernels, shards(): pl.pallas_call(functools.partial(finish_kernel, (H, D, L)), grid=(T // bl...  3.58 us

profile of v1, /device:TPU:0, one launch (start us, length us, event | category | flops | bytes accessed | tf_op | source)
XLA Modules:
  0.0 31.9 jit_solution(10017127397403924571)
XLA Ops:
  0.6 0.8 %copy.10.tab_ref = f32[64,2,21]{2,1,0:T(2,128)S(1)} copy(f32[64,2,21]{0,1,2:T(2,128)} %param.10) | data formatting | bytes 21504 | tf_op args[4]
  1.5 0.0 copy-start
  1.5 1.0 %copy-done = bf16[1024,256]{1,0:T(8,128)(2,1)S(1)} copy-done((bf16[1024,256]{1,0:T(8,128)(2,1)S(1)}, bf16[1024,256]{1,0:T(8,128)(2,1)}, u32[]{:S(2)}) %copy-start) | copy-done | bytes 524312
  2.5 0.0 copy-start.1
  2.5 1.0 %copy-done.1 = bf16[1024,256]{1,0:T(8,128)(2,1)S(1)} copy-done((bf16[1024,256]{1,0:T(8,128)(2,1)S(1)}, bf16[1024,256]{1,0:T(8,128)(2,1)}, u32[]{:S(2)}) %copy-start.1) | copy-done | bytes 524312
  3.5 0.0 copy-start.2
  3.6 1.0 %copy-done.2 = bf16[1024,256]{1,0:T(8,128)(2,1)S(1)} copy-done((bf16[1024,256]{1,0:T(8,128)(2,1)S(1)}, bf16[1024,256]{1,0:T(8,128)(2,1)}, u32[]{:S(2)}) %copy-start.2) | copy-done | bytes 524312
  4.6 0.0 copy-start.3
  4.6 1.0 %copy-done.3 = bf16[1024,256]{1,0:T(8,128)(2,1)S(1)} copy-done((bf16[1024,256]{1,0:T(8,128)(2,1)S(1)}, bf16[1024,256]{1,0:T(8,128)(2,1)}, u32[]{:S(2)}) %copy-start.3) | copy-done | bytes 524312
  5.6 0.0 copy-start.4
  5.6 0.7 %copy-done.4 = s32[1024]{0:T(1024)S(1)} copy-done((s32[1024]{0:T(1024)S(1)}, s32[1024]{0:T(1024)}, u32[]{:S(2)}) %copy-start.4) | copy-done | bytes 4120
  6.3 22.0 %main.1 = (f32[1024,256]{1,0:T(8,128)S(1)}, f32[1024,256]{1,0:T(8,128)S(1)}, f32[1024,256]{1,0:T(8,128)S(1)}, f32[1024,256]{1,0:T(8,128)S(1)}, bf16[1024,1280]{1...) custom-call(bf16[1024,256]{1,0:T(8,128)(2,1)S(1)} %copy-done.2, ...), custom_call_target="tpu_custom_call" | custom-call | tf_op jit(solution)/shard_map/main/pallas_call | solution.py:328
  28.3 3.6 %finish.1 = (f32[1024,256]{1,0:T(8,128)}, f32[1024,256]{1,0:T(8,128)}, f32[1024,256]{1,0:T(8,128)}, f32[1024,256]{1,0:T(8,128)}) custom-call(f32[1024,256]{1,0:T(8,128)S(1)} %get-tuple-element.13.lo, f32[1024,256]{1,0:T(8,128)S(1)} %get-tuple-element.14.lq, f32[1024,256]{1,0:T(8,128)S(1)} %get-tuple-element.15.lk, f32[1024,256]{1,0:T(8,128)S(1)} %get-tuple-element.16.lv, ...), custom_call_target="tpu_custom_call" | custom-call | tf_op jit(solution)/shard_map/finish/pallas_call | solution.py:369
Async XLA Ops:
  1.5 1.0 %copy-start = (bf16[1024,256]{1,0:T(8,128)(2,1)S(1)}, bf16[1024,256]{1,0:T(8,128)(2,1)}, u32[]{:S(2)}) copy-start(bf16[1024,256]{1,0:T(8,128)(2,1)} %k.1) | copy-start | bytes 1572868
  2.5 1.0 %copy-start.1 = (bf16[1024,256]{1,0:T(8,128)(2,1)S(1)}, bf16[1024,256]{1,0:T(8,128)(2,1)}, u32[]{:S(2)}) copy-start(bf16[1024,256]{1,0:T(8,128)(2,1)} %v.1) | copy-start | bytes 1572868
  3.5 1.0 %copy-start.2 = (bf16[1024,256]{1,0:T(8,128)(2,1)S(1)}, bf16[1024,256]{1,0:T(8,128)(2,1)}, u32[]{:S(2)}) copy-start(bf16[1024,256]{1,0:T(8,128)(2,1)} %q_ref.1) | copy-start | bytes 1572868
  4.6 1.0 %copy-start.3 = (bf16[1024,256]{1,0:T(8,128)(2,1)S(1)}, bf16[1024,256]{1,0:T(8,128)(2,1)}, u32[]{:S(2)}) copy-start(bf16[1024,256]{1,0:T(8,128)(2,1)} %g_ref.1) | copy-start | bytes 1572868
  5.6 0.7 %copy-start.4 = (s32[1024]{0:T(1024)S(1)}, s32[1024]{0:T(1024)}, u32[]{:S(2)}) copy-start(s32[1024]{0:T(1024)} %param.11) | copy-start | bytes 12292
